TPU v7x, 128 devices: a whole 4x4x4 slice. The times are simulated.
128 devices in a mesh: freq: 4 (over z), trace: 32 (over y, x, core).
Axes of the slice: x: 4, y: 4, z: 4, core: 2. Of those that a mesh axis runs over, the one named last changes fastest.
Arguments:
- recorded: float32 [8, 2, 2048, 4096], P(None, None, 'freq', 'trace'), may hold values from -16 to 16
- multiples: float32 [8, 2, 2048, 4096], P(None, None, 'freq', 'trace'), may hold values from -6 to 6
Outputs:
- primaries: float32 [8, 2, 2048, 4096], P(None, None, 'freq', 'trace')
- filters: float32 [8, 2, 32, 64], P(None, None, 'freq')
All inputs are finite; a program needn't handle non-finite values.
Results may differ from a plain program's by a relative error of at most 0.0001.
Values sent between devices are 32-bit elements; how exact they have to be, the bound alone decides.
No kernel may reach another device: no remote copies, remote signals or barrier semaphores. Data moves between devices by JAX's collectives and lax.ppermute only.
A program may use at most 128 MiB of HBM per device.

v0:
```python
import functools

import jax
import jax.numpy as jnp
from jax import lax
from jax.sharding import Mesh
from jax.sharding import PartitionSpec as P

FB = 64
TAPS = 64
ITERS = 3
TRACE = ("trace_0", "trace_1", "trace_2")
FREQ_TRACE = ("freq", "trace_0", "trace_1", "trace_2")


def with_halo(value, sides, width):
    for axis, dim in sides:
        size, length = (lax.axis_size(axis), value.shape[dim])
        up = [(i, (i + 1) % size) for i in range(size - 1)]
        down = [(j, i) for i, j in up]
        last = lax.slice_in_dim(value, length - width, length, axis=dim)
        first = lax.slice_in_dim(value, 0, width, axis=dim)
        before = lax.ppermute(last, axis, up)
        after = lax.ppermute(first, axis, down)
        value = jnp.concatenate([before, value, after], axis=dim)
    return value


def copy_for_each(value, axis):
    length = lax.axis_size(axis)
    return lax.all_to_all(
        jnp.broadcast_to(value[None], (length, *value.shape)), axis, 0, 0, tiled=True
    )


def of_everyone(value, axis):
    return copy_for_each(value, axis).sum(axis=0)


def by_axis(value, axes):
    return functools.reduce(lax.psum, axes, value)


def toeplitz_rows(taps_vec, trace_rows):
    tap_count = taps_vec.shape[-1]
    window_len = trace_rows + tap_count
    leading = taps_vec.shape[:-1]
    padded = jnp.concatenate(
        [
            jnp.zeros(leading + (1,), jnp.float32),
            taps_vec[..., ::-1],
            jnp.zeros(leading + (trace_rows,), jnp.float32),
        ],
        -1,
    )
    repeated = jnp.tile(padded, (1,) * len(leading) + (trace_rows,))
    return repeated[..., : trace_rows * window_len].reshape(leading + (trace_rows, window_len))


def product(left, right):
    return jnp.einsum("bfj,bxj->bfx", left, right, precision=lax.Precision.HIGHEST)


def correlate(left, right):
    return jnp.einsum("bfj,bfx->bxj", left, right, precision=lax.Precision.HIGHEST)


def forward_one(window, taps_vec):
    trace_rows = window.shape[-1] - taps_vec.shape[-1]
    toeplitz = toeplitz_rows(taps_vec, trace_rows)
    real_part = product(window[0], toeplitz[0]) - product(window[1], toeplitz[1])
    imag_part = product(window[0], toeplitz[1]) + product(window[1], toeplitz[0])
    return jnp.stack([real_part, imag_part])


def adjoint_one(window, residual, tap_count):
    real_part = correlate(window[0], residual[0]) + correlate(window[1], residual[1])
    imag_part = correlate(window[0], residual[1]) - correlate(window[1], residual[0])
    crossed = jnp.stack([real_part, imag_part])
    trace_rows, window_len = crossed.shape[-2:]
    leading = crossed.shape[:-2]
    flattened = crossed.reshape(leading + (trace_rows * window_len,))
    flattened = jnp.concatenate([flattened, jnp.zeros(leading + (trace_rows,), jnp.float32)], -1)
    column_sums = jnp.sum(flattened.reshape(leading + (trace_rows, window_len + 1)), axis=-2)
    return column_sums[..., 1 : tap_count + 1][..., ::-1]


def bending(edge_pad):
    return 2.0 * edge_pad[:, :, 1:-1] - edge_pad[:, :, :-2] - edge_pad[:, :, 2:]


def inner_sum(left, right):
    return jnp.sum(left * right, axis=(1, 2, 3))


def body(recorded, multiples):
    half_taps = TAPS // 2
    trace_rows = multiples.shape[3]
    edged = with_halo(multiples, ((TRACE, 3),), half_taps)
    shot_count, part_count, freq_rows, window_len = edged.shape
    block_count = freq_rows // FB
    windows = edged.reshape(shot_count, part_count, block_count, FB, window_len)
    trace_count = lax.axis_size(TRACE)
    weight = 0.5 * FB * trace_rows * trace_count
    residual = recorded
    shaping = jnp.zeros((shot_count, part_count, block_count, TAPS), jnp.float32)
    bent_sum = jnp.zeros_like(shaping)
    direction = shaping
    norm_now = jnp.ones((shot_count,), jnp.float32)
    for iteration in range(ITERS):
        pieces = residual.reshape(shot_count, part_count, block_count, FB, trace_rows)
        gradient = (
            of_everyone(
                lax.map(lambda paired: adjoint_one(paired[0], paired[1], TAPS), (windows, pieces)),
                TRACE,
            )
            - bent_sum
        )
        norm_next = of_everyone(inner_sum(gradient, gradient), "freq")
        if iteration == 0:
            direction = gradient
        else:
            direction = gradient + (norm_next / norm_now)[:, None, None, None] * direction
        norm_now = norm_next
        result = lax.map(lambda paired: forward_one(paired[0], paired[1]), (windows, direction))
        applied = result.reshape(shot_count, part_count, freq_rows, trace_rows)
        edge_pad = with_halo(direction, (("freq", 2),), 1)
        smooth = weight * bending(edge_pad)
        energy_sum, smooth_sum = (
            by_axis(jnp.sum(applied * applied, axis=(1, 2, 3)), FREQ_TRACE),
            by_axis(inner_sum(direction, smooth), FREQ_TRACE),
        )
        energy = energy_sum + smooth_sum / trace_count
        step_len = (norm_now / energy)[:, None, None, None]
        shaping = shaping + step_len * direction
        residual = residual - step_len * applied
        bent_sum = bent_sum + step_len * smooth
    return (residual, shaping)


def solution(mesh):
    finer = Mesh(
        mesh.devices.reshape(mesh.shape["freq"], 4, 4, 2), ("freq", "trace_0", "trace_1", "trace_2")
    )
    placed = (P(None, None, "freq", TRACE), P(None, None, "freq", TRACE))
    return jax.shard_map(
        body,
        mesh=finer,
        in_specs=placed,
        out_specs=(P(None, None, "freq", TRACE), P(None, None, "freq", None)),
        check_vma=False,
    )
```

profile of v0, /device:TPU:1, one launch (start us, length us, event | category | flops | bytes accessed | tf_op | source)
XLA Modules:
  0.0 1083.0 jit_solution(14519378353560163661)
XLA Ops:
  0.6 8.0 fusion.60
  11.4 4.5 collective-permute-start
  20.8 6.8 collective-permute-done
  30.3 4.6 collective-permute-done.1
  35.0 3.7 copy.87
  38.6 8.8 pad_maximum_fusion
  47.4 140.9 %while.60 = (s32[]{:T(128)}, f32[8,2,8,64]{3,2,1,0:T(8,128)S(1)}, f32[8,2,8,64,128]{4,3,2,1,0:T(8,128)}, f32[8,2,8,64,192]{4,3,2,1,0:T(8,128)}, s32[]{:T(128)}, /*index=5*/s32[]{:T(128)}, s32[]{}, f32[]{:T(128)}) while((s32[]{:T(128)}, f32[8,2,8,64]{3,2,1,0:T(8,128)S(1)}, f32[8,2,8,64,128]{4,3,2,1,0:T(8,128)}, ...), condition=%wide.region_2.3_spmd, body=%wide.region_0.2_spmd.sunk | while | flops 606346240 | bytes 22103216 | solution.py:114
  60.4 4.2 reshape.165
  78.0 4.2 reshape.165
  95.6 4.2 reshape.165
  113.1 4.2 reshape.165
  130.7 4.2 reshape.165
  148.3 4.2 reshape.165
  165.9 4.2 reshape.165
  183.5 4.2 reshape.165
  190.8 8.7 all-to-all-start
  199.5 17.0 %all-to-all-done = f32[32,1,8192]{2,1,0:T(1,128)S(1)} async-done(((f32[32,1,8192]{2,1,0:T(1,128)}), f32[32,1,8192]{2,1,0:T(1,128)S(1)}, u32[]{:S(2)}, u32[]{:S(2)}) %all-to-all-start) | async-done | bytes 1048608 | tf_op jit(solution)/shard_map/all_to_all | solution.py:31
  221.2 3.5 collective-permute-start.2
  228.6 120.3 %while.61 = (s32[]{:T(128)}, f32[8,2,8,64,128]{4,3,2,1,0:T(8,128)}, f32[8,2,8,64,192]{4,3,2,1,0:T(8,128)}, f32[8,2,8,64]{3,2,1,0:T(8,128)S(1)}, s32[]{:T(128)}, /*index=5*/f32[]{:T(128)}, f32[]{:T(128)}, s32[]{:T(128)}, s32[]{}) while((s32[]{:T(128)}, f32[8,2,8,64,128]{4,3,2,1,0:T(8,128)}, f32[8,2,8,64,192]{4,3,2,1,0:T(8,128)}, ...), condition=%wide.region_7.8_spmd, body=%wide.region_6.7_spmd.sunk | while | flops 604248064 | bytes 18950932 | solution.py:125
  352.3 5.5 all-to-all-start.1
  357.7 8.6 all-reduce.11
  366.4 6.5 all-reduce.8
  372.9 7.7 all-reduce.5
  380.6 8.8 all-reduce.14
  389.4 6.0 fusion.47
  395.4 141.0 %while.62 = (s32[]{:T(128)}, f32[8,2,8,64]{3,2,1,0:T(8,128)S(1)}, f32[8,2,8,64,128]{4,3,2,1,0:T(8,128)}, f32[8,2,8,64,192]{4,3,2,1,0:T(8,128)}, s32[]{:T(128)}, /*index=5*/s32[]{:T(128)}, s32[]{}, f32[]{:T(128)}) while((s32[]{:T(128)}, f32[8,2,8,64]{3,2,1,0:T(8,128)S(1)}, f32[8,2,8,64,128]{4,3,2,1,0:T(8,128)}, ...), condition=%wide.region_20.21_spmd, body=%wide.region_18.20_spmd.sunk | while | flops 606346240 | bytes 22103216 | solution.py:114
  408.8 4.2 reshape.166
  426.4 4.2 reshape.166
  443.9 4.2 reshape.166
  461.5 4.2 reshape.166
  479.1 4.2 reshape.166
  496.7 4.2 reshape.166
  514.3 4.2 reshape.166
  531.8 4.2 reshape.166
  538.9 4.2 all-to-all-start.2
  543.2 17.1 %all-to-all-done.2 = f32[32,1,8192]{2,1,0:T(1,128)S(1)} async-done(((f32[32,1,8192]{2,1,0:T(1,128)}), f32[32,1,8192]{2,1,0:T(1,128)S(1)}, u32[]{:S(2)}, u32[]{:S(2)}) %all-to-all-start.2) | async-done | bytes 1048608 | tf_op jit(solution)/shard_map/all_to_all | solution.py:31
  560.2 3.1 reduce.7
  565.2 3.2 all-to-all-start.3
  568.4 4.0 all-to-all-done.3
  578.6 120.0 %while.63 = (s32[]{:T(128)}, f32[8,2,8,64,128]{4,3,2,1,0:T(8,128)}, f32[8,2,8,64,192]{4,3,2,1,0:T(8,128)}, f32[8,2,8,64]{3,2,1,0:T(8,128)S(1)}, s32[]{:T(128)}, /*index=5*/f32[]{:T(128)}, f32[]{:T(128)}, s32[]{:T(128)}, s32[]{}) while((s32[]{:T(128)}, f32[8,2,8,64,128]{4,3,2,1,0:T(8,128)}, f32[8,2,8,64,192]{4,3,2,1,0:T(8,128)}, ...), condition=%wide.region_25.26_spmd, body=%wide.region_24.25_spmd.sunk | while | flops 604248064 | bytes 18950932 | solution.py:125
  701.4 8.7 all-reduce.10
  710.1 6.5 all-reduce.7
  716.6 7.6 all-reduce.4
  724.2 9.3 all-reduce.13
  733.5 6.0 fusion.46
  739.5 140.8 %while.64 = (s32[]{:T(128)}, f32[8,2,8,64]{3,2,1,0:T(8,128)S(1)}, f32[8,2,8,64,128]{4,3,2,1,0:T(8,128)}, f32[8,2,8,64,192]{4,3,2,1,0:T(8,128)}, s32[]{:T(128)}, /*index=5*/s32[]{:T(128)}, s32[]{}, f32[]{:T(128)}) while((s32[]{:T(128)}, f32[8,2,8,64]{3,2,1,0:T(8,128)S(1)}, f32[8,2,8,64,128]{4,3,2,1,0:T(8,128)}, ...), condition=%wide.region_38.39_spmd, body=%wide.region_36.38_spmd.sunk | while | flops 606346240 | bytes 22103216 | solution.py:114
  752.7 4.2 reshape.167
  770.3 4.2 reshape.167
  787.9 4.2 reshape.167
  805.5 4.2 reshape.167
  823.0 4.2 reshape.167
  840.6 4.2 reshape.167
  858.2 4.2 reshape.167
  875.8 4.2 reshape.167
  882.9 4.3 all-to-all-start.4
  887.2 17.1 %all-to-all-done.4 = f32[32,1,8192]{2,1,0:T(1,128)S(1)} async-done(((f32[32,1,8192]{2,1,0:T(1,128)}), f32[32,1,8192]{2,1,0:T(1,128)S(1)}, u32[]{:S(2)}, u32[]{:S(2)}) %all-to-all-start.4) | async-done | bytes 1048608 | tf_op jit(solution)/shard_map/all_to_all | solution.py:31
  904.2 3.1 reduce.8
  908.6 6.5 all_to_all.33
  921.2 119.7 %while.65 = (s32[]{:T(128)}, f32[8,2,8,64,128]{4,3,2,1,0:T(8,128)}, f32[8,2,8,64,192]{4,3,2,1,0:T(8,128)}, f32[8,2,8,64]{3,2,1,0:T(8,128)S(1)}, s32[]{:T(128)}, /*index=5*/f32[]{:T(128)}, f32[]{:T(128)}, s32[]{:T(128)}, s32[]{}) while((s32[]{:T(128)}, f32[8,2,8,64,128]{4,3,2,1,0:T(8,128)}, f32[8,2,8,64,192]{4,3,2,1,0:T(8,128)}, ...), condition=%wide.region_43.44_spmd, body=%wide.region_42.43_spmd.sunk | while | flops 604248064 | bytes 18950932 | solution.py:125
  1043.7 8.7 all-reduce.9
  1052.4 6.5 all-reduce.6
  1058.9 7.6 all-reduce.3
  1066.5 9.3 all-reduce.12
  1076.5 6.1 fusion.45
  (757 shorter events, 728.2 us)
Async XLA Ops:
  11.4 16.2 %collective-permute-start = (f32[8,2,512,32]{2,3,1,0:T(8,128)S(1)}, f32[8,2,512,32]{2,3,1,0:T(8,128)S(1)}, u32[]{:S(2)}, u32[]{:S(2)}) collective-permute-start(f32[8,2,512,32]{2,3,1,0:T(8,128)S(1)} %copy.103), channel_id=1, source_target_pairs={{0,1},{1,2},{2,3},{3,4},{4,5},{5,6},{6,7},{7,8},{8,9},{9,10},{10,1... | collective-permute-start | bytes 3145736 | tf_op jit(solution)/shard_map/ppermute | solution.py:23
  18.7 16.2 %collective-permute-start.1 = (f32[8,2,512,32]{2,3,1,0:T(8,128)S(1)}, f32[8,2,512,32]{2,3,1,0:T(8,128)}, u32[]{:S(2)}, u32[]{:S(2)}) collective-permute-start(f32[8,2,512,32]{2,3,1,0:T(8,128)S(1)} %copy.104), channel_id=1, source_target_pairs={{1,0},{2,1},{3,2},{4,3},{5,4},{6,5},{7,6},{8,7},{9,8},{10,9},{11,1... | collective-permute-start | bytes 3145736 | tf_op jit(solution)/shard_map/ppermute | solution.py:24
  190.8 25.8 %all-to-all-start = ((f32[32,1,8192]{2,1,0:T(1,128)}), f32[32,1,8192]{2,1,0:T(1,128)S(1)}, u32[]{:S(2)}, u32[]{:S(2)}) async-start(f32[32,1,8192]{2,1,0:T(1,128)} %reshape.156), calls=%async_computation | async-start | bytes 2097152 | tf_op jit(solution)/shard_map/all_to_all | solution.py:31
  221.2 130.3 %collective-permute-start.2 = (f32[8,2,1,64]{3,2,1,0:T(1,128)S(1)}, f32[8,2,1,64]{3,2,1,0:T(1,128)S(1)}, u32[]{:S(2)}, u32[]{:S(2)}) collective-permute-start(f32[8,2,1,64]{3,2,1,0:T(1,128)S(1)} %get-tuple-element.232), channel_id=1, source_target_pairs={{0,32},{32,64},{64,96},{1,33},{33,65},{65,97},{2,34},{34,66},{66,9... | collective-permute-start | bytes 12296 | tf_op jit(solution)/shard_map/ppermute | solution.py:23
  224.8 126.7 %collective-permute-start.3 = (f32[8,2,1,64]{3,2,1,0:T(1,128)S(1)}, f32[8,2,1,64]{3,2,1,0:T(1,128)S(1)}, u32[]{:S(2)}, u32[]{:S(2)}) collective-permute-start(f32[8,2,1,64]{3,2,1,0:T(1,128)S(1)} %get-tuple-element.233), channel_id=1, source_target_pairs={{32,0},{64,32},{96,64},{33,1},{65,33},{97,65},{34,2},{66,34},{98,6... | collective-permute-start | bytes 12296 | tf_op jit(solution)/shard_map/ppermute | solution.py:24
  352.3 37.1 %all-to-all-start.1 = ((f32[4,1,8]{2,1,0:T(1,128)}), f32[4,1,8]{2,1,0:T(1,128)S(1)}, u32[]{:S(2)}, u32[]{:S(2)}) async-start(f32[4,1,8]{2,1,0:T(1,128)} %broadcast_in_dim.62), calls=%async_computation.1 | async-start | bytes 4096 | tf_op jit(solution)/shard_map/all_to_all | solution.py:31
  538.9 21.3 %all-to-all-start.2 = ((f32[32,1,8192]{2,1,0:T(1,128)}), f32[32,1,8192]{2,1,0:T(1,128)S(1)}, u32[]{:S(2)}, u32[]{:S(2)}) async-start(f32[32,1,8192]{2,1,0:T(1,128)} %reshape.158), calls=%async_computation.2 | async-start | bytes 2097152 | tf_op jit(solution)/shard_map/all_to_all | solution.py:31
  565.2 7.3 all-to-all-start.3
  572.6 128.7 %collective-permute-start.4 = (f32[8,2,1,64]{3,2,1,0:T(1,128)S(1)}, f32[8,2,1,64]{3,2,1,0:T(1,128)S(1)}, u32[]{:S(2)}, u32[]{:S(2)}) collective-permute-start(f32[8,2,1,64]{3,2,1,0:T(1,128)S(1)} %get-tuple-element.230), channel_id=1, source_target_pairs={{0,32},{32,64},{64,96},{1,33},{33,65},{65,97},{2,34},{34,66},{66,9... | collective-permute-start | bytes 12296 | tf_op jit(solution)/shard_map/ppermute | solution.py:23
  574.8 126.5 %collective-permute-start.5 = (f32[8,2,1,64]{3,2,1,0:T(1,128)S(1)}, f32[8,2,1,64]{3,2,1,0:T(1,128)S(1)}, u32[]{:S(2)}, u32[]{:S(2)}) collective-permute-start(f32[8,2,1,64]{3,2,1,0:T(1,128)S(1)} %get-tuple-element.231), channel_id=1, source_target_pairs={{32,0},{64,32},{96,64},{33,1},{65,33},{97,65},{34,2},{66,34},{98,6... | collective-permute-start | bytes 12296 | tf_op jit(solution)/shard_map/ppermute | solution.py:24
  882.9 21.4 %all-to-all-start.4 = ((f32[32,1,8192]{2,1,0:T(1,128)}), f32[32,1,8192]{2,1,0:T(1,128)S(1)}, u32[]{:S(2)}, u32[]{:S(2)}) async-start(f32[32,1,8192]{2,1,0:T(1,128)} %reshape.160), calls=%async_computation.4 | async-start | bytes 2097152 | tf_op jit(solution)/shard_map/all_to_all | solution.py:31
  915.2 128.4 %collective-permute-start.6 = (f32[8,2,1,64]{3,2,1,0:T(1,128)S(1)}, f32[8,2,1,64]{3,2,1,0:T(1,128)S(1)}, u32[]{:S(2)}, u32[]{:S(2)}) collective-permute-start(f32[8,2,1,64]{3,2,1,0:T(1,128)S(1)} %get-tuple-element.228), channel_id=1, source_target_pairs={{0,32},{32,64},{64,96},{1,33},{33,65},{65,97},{2,34},{34,66},{66,9... | collective-permute-start | bytes 12296 | tf_op jit(solution)/shard_map/ppermute | solution.py:23
  917.4 126.2 %collective-permute-start.7 = (f32[8,2,1,64]{3,2,1,0:T(1,128)S(1)}, f32[8,2,1,64]{3,2,1,0:T(1,128)S(1)}, u32[]{:S(2)}, u32[]{:S(2)}) collective-permute-start(f32[8,2,1,64]{3,2,1,0:T(1,128)S(1)} %get-tuple-element.229), channel_id=1, source_target_pairs={{32,0},{64,32},{96,64},{33,1},{65,33},{97,65},{34,2},{66,34},{98,6... | collective-permute-start | bytes 12296 | tf_op jit(solution)/shard_map/ppermute | solution.py:24
where the time goes:
time: 1090 us; the launch traced here: 1080 us
  matrix products  463 us (42%)
  local copies, waits for them, and re-layouts  299 us (27%)
  other arithmetic  103 us (9%)
  blocking collectives  102 us (9%)
  waiting for transfers between devices  66.7 us (6%)
  starting transfers between devices  44.3 us (4%)
    dot_general x96, matrix products, correlate(): jnp.einsum('bfj,bfx->bxj', left, right, precision=lax.Precision.HIGHEST)  246 us
    dot_general x96, matrix products, product(): jnp.einsum('bfj,bxj->bfx', left, right, precision=lax.Precision.HIGHEST)  217 us
    reshape x24, local copies, waits for them, and re-layouts, adjoint_one(): flattened.reshape(leading + (trace_rows, window_len + 1))  102 us
    psum x12, blocking collectives, by_axis(): return functools.reduce(lax.psum, axes, value)  95.7 us
    another operation x48, local copies, waits for them, and re-layouts, toeplitz_rows(): repeated = jnp.tile(padded, (1,) * len(leading) + (trace_rows,))  57.1 us
    all_to_all x5, waiting for transfers between devices, copy_for_each(): lax.all_to_all(jnp.broadcast_to(value[None], (length, *value.shape)), axi...  55.2 us
    slice x24, local copies, waits for them, and re-layouts, forward_one(): toeplitz[0]  35.3 us
    another operation x24, other arithmetic, adjoint_one(): crossed = jnp.stack([real_part, imag_part])  30 us
  transfers between devices with their start and end apart: 13, of which 6 were waited for; matrix products, arithmetic and copies ran while one was open for 35% of the time, Pallas kernels for 0%

commit v1 on v0

v1 whole, which is shorter than its diff:
```python
import jax
import jax.numpy as jnp
from jax import lax
from jax.experimental import pallas as pl
from jax.experimental.pallas import tpu as pltpu
from jax.sharding import Mesh
from jax.sharding import PartitionSpec as P

FB = 64
TAPS = 64
ITERS = 3
HALF = 32
LANES = 128
EROWS = 32
GROWS = 8
AXES = ("z", "y", "x", "c")
TRACE = ("y", "x", "c")

f32 = jnp.float32
bf16 = jnp.bfloat16


def split(value):
    high = value.astype(bf16)
    return high, (value - high.astype(f32)).astype(bf16)


def mm(left, right):
    return lax.dot_general(left, right, (((1,), (0,)), ((), ())), preferred_element_type=f32)


def mm3(left, right):
    return mm(left[0], right[0]) + mm(left[0], right[1]) + mm(left[1], right[0])


def iota(shape, axis):
    return lax.broadcasted_iota(jnp.int32, shape, axis)


def paired(real, imag, low):
    half = LANES // 2
    if low == 0:
        top = (real, pltpu.roll(imag, half, 1))
        bottom = (imag, -pltpu.roll(real, half, 1))
    else:
        top = (pltpu.roll(real, half, 1), imag)
        bottom = (pltpu.roll(imag, half, 1), -real)
    left = iota(real.shape, 1) < half
    return jnp.concatenate([jnp.where(left, *top), jnp.where(left, *bottom)], axis=0)


def pack_kernel(flag_ref, m_ref, left_ref, right_ref, edge_ref):
    for b in range(8):
        rows = pl.ds(b * FB, FB)
        real, imag = m_ref[0, 0, rows, :], m_ref[0, 1, rows, :]
        turned = jnp.concatenate([real, imag], axis=0).T
        first, last = turned[:HALF], turned[LANES - HALF :]
        left_ref[0, b] = first
        right_ref[0, b] = last
        near = mm3(split(first), split(paired(real, imag, 0)))
        far = mm3(split(last), split(paired(real, imag, 1)))
        lane = iota(near.shape, 1) % 64
        edge_ref[0, b] = jnp.where(lane < HALF, near, far) * flag_ref[...]


def pack(flag, multiples):
    shots = multiples.shape[0]
    edge = pl.BlockSpec((1, 8, HALF, LANES), lambda s: (s, 0, 0, 0))
    shape = jax.ShapeDtypeStruct((shots, 8, HALF, LANES), f32)
    return pl.pallas_call(
        pack_kernel,
        grid=(shots,),
        in_specs=[
            pl.BlockSpec((1, LANES), lambda s: (0, 0)),
            pl.BlockSpec((1, 2, 512, LANES), lambda s: (s, 0, 0, 0)),
        ],
        out_specs=[edge, edge, edge],
        out_shape=[shape, shape, shape],
        name="pack",
    )(flag, multiples)


def diagonals(table, start, offset):
    total = None
    for g in range(table.shape[0] // 8):
        part = pltpu.roll(table[g * 8 : g * 8 + 8], (offset - start - g * 8) % LANES, 1)
        total = part if total is None else total + part
    row = iota(total.shape, 0)
    for bit in (1, 2, 4):
        total = jnp.where(row // bit % 2 == 1, pltpu.roll(total, LANES - bit, 1), total)
    return jnp.sum(total, axis=0, keepdims=True)


def corr_kernel(m_ref, r_ref, left_ref, right_ref, out_ref):
    row = iota((LANES, LANES), 0)
    lane = iota((LANES, LANES), 1)
    inner = lane % 64
    band = row - inner
    grad_mask = (band >= 1) & (band <= 64)
    auto_mask = (band >= -31) & (band <= 32)
    tail_mask = ((band <= 95) & (inner < HALF))[96:]
    for b in range(8):
        rows = pl.ds(b * FB, FB)
        real, imag = m_ref[0, 0, rows, :], m_ref[0, 1, rows, :]
        turned = jnp.concatenate([real, imag], axis=0).T
        window0 = jnp.concatenate([left_ref[0, b], turned[:96]], axis=0)
        window1 = jnp.concatenate([turned[HALF:], right_ref[0, b]], axis=0)
        streamed = split(jnp.concatenate([window0, window1], axis=1))
        rec_r, rec_i = r_ref[0, 0, rows, :], r_ref[0, 1, rows, :]
        grad_w = jnp.concatenate([paired(rec_r, rec_i, 0), paired(rec_r, rec_i, 1)], axis=0)
        auto_w = jnp.concatenate([paired(real, imag, 0), paired(real, imag, 1)], axis=0)
        table = mm3(streamed, split(jnp.concatenate([grad_w, auto_w], axis=1)))
        grad, auto = table[:, :LANES], table[:, LANES:]
        grad = jnp.where(grad_mask, grad, 0.0)
        main = jnp.where(auto_mask, auto, 0.0)
        tail = jnp.where(tail_mask, auto[96:], 0.0)
        out_ref[0, b, 0:1, :] = diagonals(grad, 0, 0)
        out_ref[0, b, 1:2, :] = diagonals(main, 0, HALF)
        out_ref[0, b, 2:3, :] = diagonals(tail, 96, HALF)
        out_ref[0, b, 3:8, :] = jnp.zeros((5, LANES), f32)


def corr(multiples, recorded, left, right):
    shots = multiples.shape[0]
    edge = pl.BlockSpec((1, 8, HALF, LANES), lambda s: (s, 0, 0, 0))
    field = pl.BlockSpec((1, 2, 512, LANES), lambda s: (s, 0, 0, 0))
    return pl.pallas_call(
        corr_kernel,
        grid=(shots,),
        in_specs=[field, field, edge, edge],
        out_specs=pl.BlockSpec((1, 8, GROWS, LANES), lambda s: (s, 0, 0, 0)),
        out_shape=jax.ShapeDtypeStruct((shots, 8, GROWS, LANES), f32),
        name="corr",
    )(multiples, recorded, left, right)


def reverse_lanes(value):
    one = ((iota((LANES, LANES), 0) + iota((LANES, LANES), 1)) % LANES == 0).astype(f32)
    return lax.dot_general(
        value, one, (((1,), (0,)), ((), ())), precision=lax.Precision.HIGHEST,
        preferred_element_type=f32,
    )


def solve_kernel(weight, blocks, grad_ref, main_ref, tail_ref, edge_ref, out_ref, dense, applied):
    lane = iota((blocks, LANES), 1)
    main = main_ref[...]
    tail = tail_ref[...]
    main_back = reverse_lanes(main)
    tail_back = reverse_lanes(tail)
    base_r = jnp.where(lane < 64, main + tail_back, main_back + tail)
    base_i = pltpu.roll(jnp.where(lane < 64, tail - main_back, main - tail_back), 64, 1)
    grad = pltpu.roll(reverse_lanes(grad_ref[...]), LANES - 1, 1)

    tap_lane = iota((TAPS, LANES), 1)
    edge_row = iota((HALF, LANES), 0)
    edge_lane = iota((HALF, LANES), 1)
    group_lane = edge_lane % HALF
    is_left = edge_lane % 64 < HALF
    for b in range(blocks):
        real = jnp.broadcast_to(base_r[b : b + 1], (TAPS, LANES))
        imag = jnp.broadcast_to(base_i[b : b + 1], (TAPS, LANES))
        real = pltpu.roll(real, 0, 1, stride=1, stride_axis=0)
        imag = pltpu.roll(imag, 64, 1, stride=1, stride_axis=0)
        edge = edge_ref[b]
        for step in (1, 2, 4, 8, 16):
            down = pltpu.roll(pltpu.roll(edge, step, 0), step, 1)
            up = pltpu.roll(pltpu.roll(edge, HALF - step, 0), LANES - step, 1)
            down_ok = is_left & (edge_row >= step) & (group_lane >= step)
            up_ok = (~is_left) & (edge_row < HALF - step) & (group_lane < HALF - step)
            edge = edge + jnp.where(down_ok, down, 0.0) + jnp.where(up_ok, up, 0.0)
        high = jnp.where(is_left, 0.0, pltpu.roll(edge, HALF, 1))
        low = pltpu.roll(pltpu.roll(edge, HALF - 1, 0), LANES - 33, 1)
        low = jnp.where((edge_row < HALF - 1) & (edge_lane % 64 < HALF - 1), low, 0.0)
        table = jnp.where(tap_lane < 64, real, imag)
        dense[b] = table - jnp.concatenate([low, high], axis=0)

    def apply(vector):
        columns = vector.T
        for b in range(blocks):
            part_r = columns[:TAPS, b : b + 1]
            part_i = columns[TAPS:, b : b + 1]
            table = dense[b]
            by_r = jnp.sum(table * part_r, axis=0, keepdims=True)
            by_i = jnp.sum(table * part_i, axis=0, keepdims=True)
            by_r = jnp.where(lane[:1] < 64, by_r, -by_r)
            applied[b : b + 1, :] = by_r + pltpu.roll(by_i, 64, 1)
        return applied[...]

    row = iota((blocks, LANES), 0)

    def bend(vector):
        before = jnp.where(row == 0, 0.0, pltpu.roll(vector, 1, 0))
        after = jnp.where(row == blocks - 1, 0.0, pltpu.roll(vector, blocks - 1, 0))
        return 2.0 * vector - before - after

    def inner(left, right):
        return jnp.sum(left * right, keepdims=True)

    direction = grad
    taps = jnp.zeros_like(grad)
    norm = inner(grad, grad)
    for step in range(ITERS):
        if step > 0:
            norm_next = inner(grad, grad)
            direction = grad + (norm_next / norm) * direction
            norm = norm_next
        smooth = weight * bend(direction)
        curved = apply(direction)
        energy = inner(direction, curved) + inner(direction, smooth)
        length = norm / energy
        taps = taps + length * direction
        grad = grad - length * (curved + smooth)
    out_ref[...] = pltpu.roll(reverse_lanes(taps), 63, 1)


def solve(weight, grad, main, tail, edge):
    blocks = grad.shape[0]
    return pl.pallas_call(
        lambda *refs: solve_kernel(weight, blocks, *refs),
        out_shape=jax.ShapeDtypeStruct((blocks, LANES), f32),
        scratch_shapes=[
            pltpu.VMEM((blocks, TAPS, LANES), f32),
            pltpu.VMEM((blocks, LANES), f32),
        ],
        name="solve",
    )(grad, main, tail, edge)


def subtract_kernel(m_ref, r_ref, left_ref, right_ref, taps_ref, out_ref, taps_out_ref):
    row = iota((LANES, LANES), 0)
    lane = iota((LANES, LANES), 1)
    spot = (row + HALF) % LANES
    band = spot - lane % 64
    mask = (band >= 1) & (band <= 64)
    half = iota((FB, LANES), 1) < 64
    for b in range(8):
        rows = pl.ds(b * FB, FB)
        field = jnp.concatenate([m_ref[0, 0, rows, :], m_ref[0, 1, rows, :]], axis=0)
        halo = jnp.concatenate(
            [jnp.zeros((64, LANES), f32), right_ref[0, b], left_ref[0, b]], axis=0
        ).T
        window0 = jnp.where(lane < 96, field, halo)
        window1 = jnp.where((lane < 64) | (lane >= 96), pltpu.roll(field, 64, 1), halo)
        streamed = jnp.concatenate(
            [
                jnp.concatenate([window0[:FB], window0[FB:]], axis=1),
                jnp.concatenate([window1[:FB], window1[FB:]], axis=1),
            ],
            axis=0,
        )
        streamed = jnp.concatenate(split(streamed), axis=0)
        taps = taps_ref[0, b : b + 1, :]
        swapped = pltpu.roll(taps, 64, 1)
        swapped = jnp.where(lane[:1] < 64, -swapped, swapped)
        top = jnp.broadcast_to(taps, (LANES, LANES))
        bottom = jnp.broadcast_to(swapped, (LANES, LANES))
        top = pltpu.roll(top, 96, 1, stride=1, stride_axis=0)
        bottom = pltpu.roll(bottom, 96, 1, stride=1, stride_axis=0)
        weights = jnp.concatenate(
            [jnp.where(mask, top, 0.0), jnp.where(mask, bottom, 0.0)], axis=0
        )
        weights = jnp.concatenate(split(weights), axis=1)
        made = mm(streamed, weights)
        made = (made[:LANES, :LANES] + made[LANES:, :LANES]) + (
            made[:LANES, LANES:] + made[LANES:, LANES:]
        )
        made0, made1 = made[:FB], made[FB:]
        real = jnp.where(half, made0, pltpu.roll(made1, 64, 1))
        imag = jnp.where(half, pltpu.roll(made0, 64, 1), made1)
        out_ref[0, 0, rows, :] = r_ref[0, 0, rows, :] - real
        out_ref[0, 1, rows, :] = r_ref[0, 1, rows, :] - imag
    taps_out_ref[0, 0] = taps_ref[0, :, :TAPS]
    taps_out_ref[0, 1] = taps_ref[0, :, TAPS:]


def subtract(multiples, recorded, left, right, taps):
    shots = multiples.shape[0]
    edge = pl.BlockSpec((1, 8, HALF, LANES), lambda s: (s, 0, 0, 0))
    field = pl.BlockSpec((1, 2, 512, LANES), lambda s: (s, 0, 0, 0))
    return pl.pallas_call(
        subtract_kernel,
        grid=(shots,),
        in_specs=[field, field, edge, edge, pl.BlockSpec((1, 8, LANES), lambda s: (s, 0, 0))],
        out_specs=[field, pl.BlockSpec((1, 2, 8, TAPS), lambda s: (s, 0, 0, 0))],
        out_shape=[
            jax.ShapeDtypeStruct(recorded.shape, f32),
            jax.ShapeDtypeStruct((shots, 2, 8, TAPS), f32),
        ],
        name="subtract",
    )(multiples, recorded, left, right, taps)


def body(recorded, multiples):
    shots = multiples.shape[0]
    y, x, c = (lax.axis_index(name) for name in TRACE)
    place = (y * 4 + x) * 2 + c
    lane = jnp.arange(LANES)[None] % 64
    flag = jnp.where(lane < HALF, place == 0, place == 31).astype(f32)
    first, last, edge = pack(flag, multiples)
    up = [(i, i + 1) for i in range(31)]
    left = lax.ppermute(last, TRACE, up)
    right = lax.ppermute(first, TRACE, [(j, i) for i, j in up])
    sums = corr(multiples, recorded, left, right)

    payload = jnp.concatenate([sums, edge], axis=2).reshape(2, shots // 2, 8, -1, LANES)
    mine = lax.dynamic_index_in_dim(payload, c, 0, keepdims=False)
    other = lax.dynamic_index_in_dim(payload, 1 - c, 0, keepdims=False)
    mine = mine + lax.ppermute(other, "c", [(0, 1), (1, 0)])
    rows = GROWS + EROWS
    mine = mine.reshape(16, 2 * rows, LANES)
    owned = lax.all_to_all(mine, ("y", "x"), 0, 0, tiled=True).sum(axis=0)
    shot = lax.all_to_all(
        jnp.broadcast_to(owned[None], (16, 2 * rows, LANES)), ("z", "x"), 0, 0, tiled=True
    ).reshape(32, rows, LANES)
    weight = 0.5 * FB * 4096
    taps = solve(weight, shot[:, 0], shot[:, 1], shot[:, 2], shot[:, GROWS:])
    taps = lax.dynamic_slice_in_dim(taps, lax.axis_index("z") * 8, 8, 0)
    taps = lax.all_to_all(
        jnp.broadcast_to(taps[None], (8, 8, LANES)), ("c", "y"), 0, 0, tiled=True
    )
    return tuple(subtract(multiples, recorded, left, right, taps))


def solution(mesh):
    finer = Mesh(mesh.devices.reshape(4, 4, 4, 2), AXES)
    placed = P(None, None, "z", TRACE)
    return jax.shard_map(
        body,
        mesh=finer,
        in_specs=(placed, placed),
        out_specs=(placed, P(None, None, "z", None)),
        check_vma=False,
    )
```

time: 1090 us -> 153 us (0.14)
  matrix products: 463 us -> 0 us
  local copies, waits for them, and re-layouts: 299 us -> 4.16 us
  other arithmetic: 103 us -> 1.68 us
  Pallas kernels: 0 us -> 74.8 us
  blocking collectives: 102 us -> 31.2 us
  waiting for transfers between devices: 66.7 us -> 27.9 us
  starting transfers between devices: 44.3 us -> 12.1 us
    dot_general x192 -> x0, matrix products: 463 us -> none  [the longest x96 246 us: correlate(): jnp.einsum('bfj,bfx->bxj', left, right, precision=lax.Precision.HIGHEST)]
    reshape x24 -> x0, local copies, waits for them, and re-layouts: 102 us -> none  [adjoint_one(): flattened.reshape(leading + (trace_rows, window_len + 1))]
    psum x12 -> x0, blocking collectives: 95.7 us -> none  [by_axis(): return functools.reduce(lax.psum, axes, value)]
    another operation x126 -> x0, local copies, waits for them, and re-layouts: 83.8 us -> none  [the longest x48 57.1 us: toeplitz_rows(): repeated = jnp.tile(padded, (1,) * len(leading) + (trace_rows,))]
    pallas_call x0 -> x4, Pallas kernels: none -> 74.8 us  [the longest x1 29.7 us: corr(): pl.pallas_call(corr_kernel, grid=(shots,), in_specs=[field, field, edge,...]
    all_to_all x5 -> x1, waiting for transfers between devices: 55.2 us -> 11.4 us  [body(): lax.all_to_all(jnp.broadcast_to(owned[None], (16, 2 * rows, LANES)), ('z'...]
    slice x52 -> x2, local copies, waits for them, and re-layouts: 45.1 us -> 1.5 us  [body(): taps = solve(weight, shot[:, 0], shot[:, 1], shot[:, 2], shot[:, GROWS:])]
    another operation x24 -> x0, other arithmetic: 30 us -> none  [adjoint_one(): crossed = jnp.stack([real_part, imag_part])]
  transfers between devices with their start and end apart: 13 -> 4, of which waited for: 6 -> 4; matrix products, arithmetic and copies ran while one was open for 35% -> 0% of each run, Pallas kernels for 0% -> 0%
where the time goes in v1:
time: 153 us
  Pallas kernels  74.8 us (49%)
  blocking collectives  31.2 us (20%)
  waiting for transfers between devices  27.9 us (18%)
  starting transfers between devices  12.1 us (8%)
  local copies, waits for them, and re-layouts  4.16 us (3%)
  other arithmetic  1.68 us (1%)
    pallas_call x1, Pallas kernels, corr(): pl.pallas_call(corr_kernel, grid=(shots,), in_specs=[field, field, edge,...  29.7 us
    pallas_call x1, Pallas kernels, solve(): pl.pallas_call(lambda *refs: solve_kernel(weight, blocks, *refs), out_sha...  22.3 us
    all_to_all x1, blocking collectives, body(): owned = lax.all_to_all(mine, ('y', 'x'), 0, 0, tiled=True).sum(axis=0)  20.7 us
    pallas_call x1, Pallas kernels, subtract(): pl.pallas_call(subtract_kernel, grid=(shots,), in_specs=[field, field, ed...  14.5 us
    all_to_all x1, waiting for transfers between devices, body(): lax.all_to_all(jnp.broadcast_to(owned[None], (16, 2 * rows, LANES)), ('z'...  11.4 us
    all_to_all x1, blocking collectives, body(): lax.all_to_all(jnp.broadcast_to(taps[None], (8, 8, LANES)), ('c', 'y'), 0...  10.4 us
    ppermute x1, waiting for transfers between devices, body(): left = lax.ppermute(last, TRACE, up)  10.1 us
    pallas_call x1, Pallas kernels, pack(): pl.pallas_call(pack_kernel, grid=(shots,), in_specs=[pl.BlockSpec((1, LAN...  8.29 us
  transfers between devices with their start and end apart: 4, of which 4 were waited for; matrix products, arithmetic and copies ran while one was open for 0% of the time, Pallas kernels for 0%

profile of v1, /device:TPU:1, one launch (start us, length us, event | category | flops | bytes accessed | tf_op | source)
XLA Modules:
  0.0 152.5 jit_solution(16974184429715863511)
XLA Ops:
  0.6 0.5 select_convert_fusion.flag_ref
  1.2 8.3 %pack.1 = (f32[8,8,32,128]{3,2,1,0:T(8,128)}, f32[8,8,32,128]{3,2,1,0:T(8,128)}, f32[8,8,32,128]{3,2,1,0:T(8,128)}) custom-call(f32[1,128]{1,0:T(1,128)} %select_convert_fusion.flag_ref, f32[8,2,512,128]{3,2,1,0:T(8,128)} %m_ref.5), custom_call_target="tpu_custom_call" | custom-call | tf_op jit(solution)/shard_map/pack/pallas_call | solution.py:70
  9.5 4.5 %collective-permute-start = (f32[8,8,32,128]{3,2,1,0:T(8,128)}, f32[8,8,32,128]{3,2,1,0:T(8,128)S(1)}, u32[]{:S(2)}, u32[]{:S(2)}) collective-permute-start(f32[8,8,32,128]{3,2,1,0:T(8,128)} %get-tuple-element.5), channel_id=1, source_target_pairs={{0,1},{1,2},{2,3},{3,4},{4,5},{5,6},{6,7},{7,8},{8,9},{9,10},{10,1... | collective-permute-start | bytes 3145736 | tf_op jit(solution)/shard_map/ppermute | solution.py:302
  13.9 1.9 %collective-permute-start.1 = (f32[8,8,32,128]{3,2,1,0:T(8,128)}, f32[8,8,32,128]{3,2,1,0:T(8,128)S(1)}, u32[]{:S(2)}, u32[]{:S(2)}) collective-permute-start(f32[8,8,32,128]{3,2,1,0:T(8,128)} %get-tuple-element.6), channel_id=1, source_target_pairs={{1,0},{2,1},{3,2},{4,3},{5,4},{6,5},{7,6},{8,7},{9,8},{10,9},{11,1... | collective-permute-start | bytes 3145736 | tf_op jit(solution)/shard_map/ppermute | solution.py:303
  15.9 0.0 copy-start.2
  15.9 10.1 %collective-permute-done.left_ref = f32[8,8,32,128]{3,2,1,0:T(8,128)S(1)} collective-permute-done((f32[8,8,32,128]{3,2,1,0:T(8,128)}, f32[8,8,32,128]{3,2,1,0:T(8,128)S(1)}, u32[]{:S(2)}, u32[]{:S(2)}) %collective-permute-start) | collective-permute-done | bytes 1048608 | tf_op jit(solution)/shard_map/ppermute | solution.py:302
  26.0 0.0 copy-start
  26.0 4.3 %collective-permute-done.1.right_ref = f32[8,8,32,128]{3,2,1,0:T(8,128)S(1)} collective-permute-done((f32[8,8,32,128]{3,2,1,0:T(8,128)}, f32[8,8,32,128]{3,2,1,0:T(8,128)S(1)}, u32[]{:S(2)}, u32[]{:S(2)}) %collective-permute-start.1) | collective-permute-done | bytes 1048608 | tf_op jit(solution)/shard_map/ppermute | solution.py:303
  30.3 0.0 copy-done
  30.3 0.0 copy-start.1
  30.3 1.0 copy-done.1
  31.3 29.7 %corr.1 = f32[8,8,8,128]{3,2,1,0:T(8,128)} custom-call(f32[8,2,512,128]{3,2,1,0:T(8,128)} %m_ref.5, f32[8,2,512,128]{3,2,1,0:T(8,128)} %r_ref.3, f32[8,8,32,128]{3,2,1,0:T(8,128)} %copy-done, f32[8,8,32,128]{3,2,1,0:T(8,128)} %copy-done.1), custom_call_target="tpu_custom_call" | custom-call | tf_op jit(solution)/shard_map/corr/pallas_call | solution.py:127
  61.0 0.0 copy-done.2
  61.1 1.1 pad_maximum_fusion
  62.1 0.1 dynamic-slice_bitcast_fusion
  62.2 0.1 collective-permute-start.2
  62.3 2.1 %collective-permute-done.2 = f32[4,8,40,128]{3,2,1,0:T(8,128)S(1)} collective-permute-done((f32[4,8,40,128]{3,2,1,0:T(8,128)S(1)}, f32[4,8,40,128]{3,2,1,0:T(8,128)S(1)}, u32[]{:S(2)}, u32[]{:S(2)}) %collective-permute-start.2) | collective-permute-done | bytes 655392 | tf_op jit(solution)/shard_map/ppermute | solution.py:309
  64.4 0.1 bitcast_add_fusion
  64.4 20.7 %all_to_all.15 = f32[16,80,128]{2,1,0:T(8,128)S(1)} all-to-all(f32[16,80,128]{2,1,0:T(8,128)S(1)} %bitcast.12), channel_id=1, replica_groups=mesh['z'=4,'y'=4,'x'=4,'c'=2] {'y','x'}, dimensions={0} | all-to-all | bytes 1310720 | tf_op jit(solution)/shard_map/all_to_all | solution.py:312
  85.2 0.9 broadcast_in_dim.23
  86.1 5.7 %all-to-all-start.1 = ((f32[16,80,128]{2,1,0:T(8,128)}), f32[16,80,128]{2,1,0:T(8,128)S(1)}, u32[]{:S(2)}, u32[]{:S(2)}) async-start(f32[16,80,128]{2,1,0:T(8,128)} %broadcast_in_dim.23), calls=%async_computation.1 | async-start | bytes 1310720 | tf_op jit(solution)/shard_map/all_to_all | solution.py:313
  91.8 11.4 %all-to-all-done.1 = f32[16,80,128]{2,1,0:T(8,128)S(1)} async-done(((f32[16,80,128]{2,1,0:T(8,128)}), f32[16,80,128]{2,1,0:T(8,128)S(1)}, u32[]{:S(2)}, u32[]{:S(2)}) %all-to-all-start.1) | async-done | bytes 655392 | tf_op jit(solution)/shard_map/all_to_all | solution.py:313
  103.2 0.6 fusion
  103.8 0.9 slice.19.refs_3_
  104.7 22.3 %solve.1 = f32[32,128]{1,0:T(8,128)} custom-call(f32[32,128]{1,0:T(8,128)} %bitcast.17, f32[32,128]{1,0:T(8,128)} %bitcast.16, f32[32,128]{1,0:T(8,128)} %bitcast.15, f32[32,32,128]{2,1,0:T(8,128)} %slice.19.refs_3_), custom_call_target="tpu_custom_call" | custom-call | tf_op jit(solution)/shard_map/solve/pallas_call | solution.py:219
  126.9 0.7 constant_dynamic-slice_fusion
  127.6 10.4 %all_to_all.16.taps_ref = f32[8,8,128]{2,1,0:T(8,128)} all-to-all(f32[8,8,128]{2,1,0:T(8,128)S(1)} %broadcast_in_dim.24), channel_id=1, replica_groups=mesh['z'=4,'y'=4,'x'=4,'c'=2] {'c','y'}, dimensions={0} | all-to-all | bytes 65536 | tf_op jit(solution)/shard_map/all_to_all | solution.py:319
  138.0 14.5 %subtract.2 = (f32[8,2,512,128]{3,2,1,0:T(8,128)}, f32[8,2,8,64]{3,2,1,0:T(8,128)}) custom-call(f32[8,2,512,128]{3,2,1,0:T(8,128)} %m_ref.5, f32[8,2,512,128]{3,2,1,0:T(8,128)} %r_ref.3, f32[8,8,32,128]{3,2,1,0:T(8,128)} %copy-done, f32[8,8,32,128]{3,2,1,0:T(8,128)} %copy-done.1, f32[8,8,128]{2,1,0:T(8,128)} %all_to_all.16.taps_ref), custom_call_target="tpu_custom_call" | custom-call | tf_op jit(solution)/shard_map/subtract/pallas_call | solution.py:281
  (2 shorter events, 0.0 us)
Async XLA Ops:
  9.5 16.5 %collective-permute-start = (f32[8,8,32,128]{3,2,1,0:T(8,128)}, f32[8,8,32,128]{3,2,1,0:T(8,128)S(1)}, u32[]{:S(2)}, u32[]{:S(2)}) collective-permute-start(f32[8,8,32,128]{3,2,1,0:T(8,128)} %get-tuple-element.5), channel_id=1, source_target_pairs={{0,1},{1,2},{2,3},{3,4},{4,5},{5,6},{6,7},{7,8},{8,9},{9,10},{10,1... | collective-permute-start | bytes 3145736 | tf_op jit(solution)/shard_map/ppermute | solution.py:302
  13.9 16.3 %collective-permute-start.1 = (f32[8,8,32,128]{3,2,1,0:T(8,128)}, f32[8,8,32,128]{3,2,1,0:T(8,128)S(1)}, u32[]{:S(2)}, u32[]{:S(2)}) collective-permute-start(f32[8,8,32,128]{3,2,1,0:T(8,128)} %get-tuple-element.6), channel_id=1, source_target_pairs={{1,0},{2,1},{3,2},{4,3},{5,4},{6,5},{7,6},{8,7},{9,8},{10,9},{11,1... | collective-permute-start | bytes 3145736 | tf_op jit(solution)/shard_map/ppermute | solution.py:303
  15.9 45.2 %copy-start.2 = (f32[8,8,32,128]{3,2,1,0:T(8,128)S(1)}, f32[8,8,32,128]{3,2,1,0:T(8,128)}, u32[]{:S(2)}) copy-start(f32[8,8,32,128]{3,2,1,0:T(8,128)} %get-tuple-element.7) | copy-start | bytes 3145732
  26.0 4.3 %copy-start = (f32[8,8,32,128]{3,2,1,0:T(8,128)}, f32[8,8,32,128]{3,2,1,0:T(8,128)S(1)}, u32[]{:S(2)}) copy-start(f32[8,8,32,128]{3,2,1,0:T(8,128)S(1)} %collective-permute-done.left_ref) | copy-start | bytes 3145732
  30.3 1.0 copy-start.1
  62.2 2.2 %collective-permute-start.2 = (f32[4,8,40,128]{3,2,1,0:T(8,128)S(1)}, f32[4,8,40,128]{3,2,1,0:T(8,128)S(1)}, u32[]{:S(2)}, u32[]{:S(2)}) collective-permute-start(f32[4,8,40,128]{3,2,1,0:T(8,128)S(1)} %dynamic-slice_bitcast_fusion), channel_id=1, source_target_pairs={{0,1},{1,0},{2,3},{3,2},{4,5},{5,4},{6,7},{7,6},{8,9},{9,8},{10,11... | collective-permute-start | bytes 1966088 | tf_op jit(solution)/shard_map/ppermute | solution.py:309
  86.1 17.1 %all-to-all-start.1 = ((f32[16,80,128]{2,1,0:T(8,128)}), f32[16,80,128]{2,1,0:T(8,128)S(1)}, u32[]{:S(2)}, u32[]{:S(2)}) async-start(f32[16,80,128]{2,1,0:T(8,128)} %broadcast_in_dim.23), calls=%async_computation.1 | async-start | bytes 1310720 | tf_op jit(solution)/shard_map/all_to_all | solution.py:313

commit v2 on v1

v2 whole, which is shorter than its diff:
```python
import jax
import jax.numpy as jnp
from jax import lax
from jax.experimental import pallas as pl
from jax.experimental.pallas import tpu as pltpu
from jax.sharding import Mesh
from jax.sharding import PartitionSpec as P


FB = 64
TAPS = 64
ITERS = 3
HALF = 32
LANES = 128
AXES = ("z", "y", "x", "c")
TRACE = ("y", "x", "c")

f32 = jnp.float32
bf16 = jnp.bfloat16


def split(value):
    high = value.astype(bf16)
    return high, (value - high.astype(f32)).astype(bf16)


def mm(left, right):
    return lax.dot_general(left, right, (((1,), (0,)), ((), ())), preferred_element_type=f32)


def iota(shape, axis):
    return lax.broadcasted_iota(jnp.int32, shape, axis)


def mm_t(left, right):
    return lax.dot_general(left, right, (((1,), (1,)), ((), ())), preferred_element_type=f32)


def exact(left, right, dims):
    return lax.dot_general(
        left, right, (dims, ((), ())), precision=lax.Precision.HIGHEST,
        preferred_element_type=f32,
    )


def field_spec(first=0):
    return pl.BlockSpec((1, 2, 512, LANES), lambda s: (s + first, 0, 0, 0))


def edge_spec():
    return pl.BlockSpec((1, 8, HALF, LANES), lambda s: (s, 0, 0, 0))


def pack_kernel(m_ref, left_ref, right_ref):
    for shot in range(2):
        for b in range(8):
            rows = pl.ds(b * FB, FB)
            turned = jnp.concatenate(
                [m_ref[shot, 0, rows, :], m_ref[shot, 1, rows, :]], axis=0
            ).T
            left_ref[shot, b] = turned[:HALF]
            right_ref[shot, b] = turned[LANES - HALF :]


def pack(first, shots, multiples):
    shape = jax.ShapeDtypeStruct((shots, 8, HALF, LANES), f32)
    edge = pl.BlockSpec((2, 8, HALF, LANES), lambda s: (s, 0, 0, 0))
    return pl.pallas_call(
        pack_kernel,
        grid=(shots // 2,),
        in_specs=[pl.BlockSpec((2, 2, 512, LANES), lambda s: (s + first // 2, 0, 0, 0))],
        out_specs=[edge, edge],
        out_shape=[shape, shape],
        name="pack",
    )(multiples)


def edges_side(shots, is_left, edge_ref, out_ref):
    lane = iota((HALF, LANES), 1)
    home = (lane % 64 >= HALF) if is_left else (lane % 64 < HALF)
    spot = lane % HALF
    sign = jnp.where(lane < 64, 1.0, -1.0)

    def load(shot, b):
        if is_left:
            return edge_ref[shot, b]
        return jnp.concatenate(
            [edge_ref[shot, b, 1:, :], jnp.zeros((1, LANES), f32)], axis=0
        )

    def one(pair, carry):
        spots = [(pair * 2 + k, b) for k in range(2) for b in range(0, 8, 2)]
        tables = []
        for shot, b in spots:
            here, there = load(shot, b), load(shot, b + 1)
            here_turn = pltpu.roll(here, 64, 1) * sign
            there_turn = pltpu.roll(there, 64, 1) * sign
            if is_left:
                against = [there, here, there_turn, here_turn]
            else:
                against = [here, there, here_turn, there_turn]
            against = split(jnp.concatenate(against, axis=0))
            rows = split(jnp.concatenate([here, there], axis=0))
            made = (
                mm_t(rows[0], against[0]) + mm_t(rows[0], against[1]) + mm_t(rows[1], against[0])
            )
            tables.append(jnp.where(home, made[:HALF], made[HALF:]))
        for step in (1, 2, 4, 8, 16):
            fill = jnp.zeros((step, LANES), f32)
            inside = (spot >= step) if is_left else (spot < HALF - step)
            for k, table in enumerate(tables):
                if is_left:
                    moved = jnp.concatenate([fill, pltpu.roll(table, step, 1)[:-step]], axis=0)
                else:
                    moved = jnp.concatenate(
                        [pltpu.roll(table, LANES - step, 1)[step:], fill], axis=0
                    )
                tables[k] = table + jnp.where(inside, moved, 0.0)
        for (shot, b), table in zip(spots, tables):
            out_ref[shot, b] = jnp.where(home, table, 0.0)
            other = pltpu.roll(table, HALF if is_left else LANES - HALF, 1)
            out_ref[shot, b + 1] = jnp.where(home, other, 0.0)
        return carry

    lax.fori_loop(0, shots // 2, one, 0)


def edges_kernel(shots, on_ref, left_ref, right_ref, out_ref):
    @pl.when(on_ref[0] == 0)
    def _():
        out_ref[...] = jnp.zeros_like(out_ref)

    @pl.when(on_ref[0] == 1)
    def _():
        edges_side(shots, True, left_ref, out_ref)

    @pl.when(on_ref[0] == 2)
    def _():
        edges_side(shots, False, right_ref, out_ref)


def edges(on, first, last):
    shots = first.shape[0]
    return pl.pallas_call(
        lambda *refs: edges_kernel(shots, *refs),
        in_specs=[pl.BlockSpec(memory_space=pltpu.SMEM)]
        + [pl.BlockSpec(memory_space=pltpu.VMEM)] * 2,
        out_shape=jax.ShapeDtypeStruct((shots, 8, HALF, LANES), f32),
        name="edges",
    )(on, first, last)


def corr_kernel(shots, m_ref, r_ref, left_ref, right_ref, out_ref, high, low, w_high, w_low, acc):
    shot = pl.program_id(0)
    for b in range(8):
        rows = pl.ds(b * FB, FB)
        turned = jnp.concatenate([m_ref[0, 0, rows, :], m_ref[0, 1, rows, :]], axis=0).T
        for part, at in ((left_ref[0, b], 0), (turned, HALF), (right_ref[0, b], HALF + LANES)):
            part_high, part_low = split(part)
            high[b, pl.ds(at, part.shape[0]), :] = part_high
            low[b, pl.ds(at, part.shape[0]), :] = part_low
    left = iota((FB, LANES), 1) < 64
    for b in range(8):
        rows = pl.ds(b * FB, FB)
        for ref, at in ((r_ref, 0), (m_ref, LANES)):
            real, imag = ref[0, 0, rows, :], ref[0, 1, rows, :]
            real_turn, imag_turn = pltpu.roll(real, 64, 1), pltpu.roll(imag, 64, 1)
            pieces = (
                jnp.where(left, real, imag_turn),
                jnp.where(left, imag, -real_turn),
                jnp.where(left, real_turn, imag),
                jnp.where(left, imag_turn, -real),
            )
            for k, piece in enumerate(pieces):
                piece_high, piece_low = split(piece)
                w_high[b, pl.ds(k * FB, FB), pl.ds(at, LANES)] = piece_high
                w_low[b, pl.ds(k * FB, FB), pl.ds(at, LANES)] = piece_low
    row = iota((LANES, LANES), 0)
    inner = iota((LANES, LANES), 1) % 64
    band = row - inner
    grad_mask = (band >= 1) & (band <= 64)
    auto_mask = (band >= -31) & (band <= 32)
    tail_mask = ((band <= 95) & (inner < HALF))[96:]
    for b in range(8):
        lead = jnp.concatenate([high[b, 0:128, :], high[b, 64:192, :]], axis=1)
        rest = jnp.concatenate([low[b, 0:128, :], low[b, 64:192, :]], axis=1)
        table = mm(lead, w_high[b]) + mm(lead, w_low[b]) + mm(rest, w_high[b])
        grad, auto = table[:, :LANES], table[:, LANES:]
        for kind, part, mask, start, offset in (
            (0, grad, grad_mask, 0, 0),
            (1, auto, auto_mask, 0, HALF),
            (2, auto[96:], tail_mask, 96, HALF),
        ):
            part = jnp.where(mask, part, 0.0)
            total = None
            for g in range(part.shape[0] // 8):
                piece = pltpu.roll(part[g * 8 : g * 8 + 8], (offset - start - g * 8) % LANES, 1)
                total = piece if total is None else total + piece
            acc[kind, pl.ds(shot * 8 + b, 1)] = total[None]

    @pl.when(shot == shots - 1)
    def _():
        count = shots * 8
        sums = []
        for kind in range(3):
            total = acc[kind].reshape(count * 8, LANES)
            level = iota(total.shape, 0)
            for bit in (1, 2, 4):
                total = jnp.where(level // bit % 2 == 1, pltpu.roll(total, LANES - bit, 1), total)
            sums.append(jnp.sum(total.reshape(count, 8, LANES), axis=1))
        flip = ((iota((LANES, LANES), 0) + iota((LANES, LANES), 1)) % LANES == 0).astype(f32)
        flip = jnp.where(iota((LANES, LANES), 0) < 64, -flip, flip)
        auto = sums[1] + exact(sums[2], flip, ((1,), (0,)))
        for k in range(shots):
            out_ref[k, 0:8, :] = sums[0][k * 8 : k * 8 + 8]
            out_ref[k, 8:16, :] = auto[k * 8 : k * 8 + 8]


def corr(first, shots, multiples, recorded, left, right):
    return pl.pallas_call(
        lambda *refs: corr_kernel(shots, *refs),
        grid=(shots,),
        in_specs=[field_spec(first), field_spec(first), edge_spec(), edge_spec()],
        out_specs=pl.BlockSpec((shots, 16, LANES), lambda s: (0, 0, 0)),
        out_shape=jax.ShapeDtypeStruct((shots, 16, LANES), f32),
        scratch_shapes=[
            pltpu.VMEM((8, 192, LANES), bf16),
            pltpu.VMEM((8, 192, LANES), bf16),
            pltpu.VMEM((8, 256, 256), bf16),
            pltpu.VMEM((8, 256, 256), bf16),
            pltpu.VMEM((3, shots * 8, 8, LANES), f32),
        ],
        name="corr",
    )(multiples, recorded, left, right)


def solve_kernel(weight, z_ref, *refs):
    sums_refs, (out_ref, lags, table, vec) = refs[:4], refs[4:]
    grad_rows = jnp.concatenate([ref[0:8, :] for ref in sums_refs], axis=0)
    auto_rows = jnp.concatenate([ref[8:16, :] for ref in sums_refs], axis=0)
    turn = lambda value: pltpu.roll(value, 64, 1)
    lane = iota((TAPS, LANES), 1)
    row = iota((TAPS, LANES), 0)
    group = lane // HALF
    place = lane % HALF
    block = (place + z_ref[0] * 8) % HALF
    stacked = jnp.concatenate(
        [grad_rows, turn(grad_rows), turn(grad_rows), grad_rows], axis=0
    )
    pick = (lane == LANES - 1 - row).astype(f32)
    grad = exact(pick, stacked, ((1,), (1,)))
    lag = iota((LANES, LANES), 0) - 64
    pick = (iota((LANES, LANES), 1) == jnp.abs(lag)).astype(f32)
    stacked = jnp.concatenate(
        [auto_rows, turn(auto_rows), auto_rows, turn(auto_rows)], axis=0
    )
    made = exact(pick, stacked, ((1,), (1,)))
    odd = iota((LANES, LANES), 1) // HALF % 2 == 1
    lags[0:LANES, :] = jnp.where(odd & (lag < 0), -made, made)
    for a in range(HALF):
        part = jnp.concatenate(
            [ref[pl.ds(16 + a * 8, 8), :] for ref in sums_refs], axis=0
        )
        other = turn(part)
        turned = jnp.concatenate([part, other, part, other], axis=0).T
        table[a] = turned[:TAPS]

    flip = jnp.where(group == 3, -1.0, 1.0)
    even = group % 2 == 0

    def apply(vector):
        vec[...] = vector
        total = jnp.zeros((TAPS, LANES), f32)
        for k in range(TAPS):
            total = total + lags[64 - k : 128 - k, :] * vec[k : k + 1, :]
        low = jnp.zeros((HALF, LANES), f32)
        high = jnp.zeros((HALF, LANES), f32)
        for a in range(HALF):
            low = low + table[a, :HALF] * vec[a : a + 1, :]
            high = high + table[a, HALF:] * vec[HALF + a : HALF + a + 1, :]
        total = (total - jnp.concatenate([low, high], axis=0)) * flip
        total = total + pltpu.roll(total, LANES - HALF, 1)
        return jnp.where(even, total, pltpu.roll(total, LANES - HALF, 1))

    def bend(vector):
        before = jnp.where(place == 0, pltpu.roll(vector, 97, 1), pltpu.roll(vector, 1, 1))
        after = jnp.where(
            place == HALF - 1, pltpu.roll(vector, 31, 1), pltpu.roll(vector, 127, 1)
        )
        before = jnp.where(block == 0, 0.0, before)
        after = jnp.where(block == HALF - 1, 0.0, after)
        return 2.0 * vector - before - after

    def inner(left, right):
        return 0.5 * jnp.sum(left * right, keepdims=True)

    direction = grad
    taps = jnp.zeros_like(grad)
    norm = inner(grad, grad)
    for step in range(ITERS):
        if step > 0:
            norm_next = inner(grad, grad)
            direction = grad + (norm_next / norm) * direction
            norm = norm_next
        bent = apply(direction) + weight * bend(direction)
        length = norm / inner(direction, bent)
        taps = taps + length * direction
        grad = grad - length * bent
    pick = ((iota((TAPS, LANES), 1) % 64) == TAPS - 1 - row).astype(f32)
    made = exact(taps, pick, ((0,), (0,)))
    out_ref[...] = jnp.where(iota((8, LANES), 1) < 64, made[:8], made[HALF : HALF + 8])


def solve(weight, z, parts):
    return pl.pallas_call(
        lambda *refs: solve_kernel(weight, *refs),
        in_specs=[pl.BlockSpec(memory_space=pltpu.SMEM)]
        + [pl.BlockSpec(memory_space=pltpu.VMEM)] * 4,
        out_shape=jax.ShapeDtypeStruct((8, LANES), f32),
        scratch_shapes=[
            pltpu.VMEM((LANES, LANES), f32),
            pltpu.VMEM((HALF, TAPS, LANES), f32),
            pltpu.VMEM((TAPS, LANES), f32),
        ],
        name="solve",
    )(z, *parts)


def subtract_kernel(
    m_ref, r_ref, left_ref, right_ref, taps_ref, out_ref, taps_out_ref, lead, weights
):
    lane = iota((LANES, LANES), 1)
    for b in range(8):
        rows = pl.ds(b * FB, FB)
        field = jnp.concatenate([m_ref[0, 0, rows, :], m_ref[0, 1, rows, :]], axis=0)
        halo = jnp.concatenate(
            [jnp.zeros((64, LANES), f32), right_ref[0, b], left_ref[0, b]], axis=0
        ).T
        window0 = jnp.where(lane < 96, field, halo)
        window1 = jnp.where((lane < 64) | (lane >= 96), pltpu.roll(field, 64, 1), halo)
        for j, window in enumerate((window0, window1)):
            for k, part in enumerate(split(window)):
                at = pl.ds(k * LANES + j * FB, FB)
                lead[b, at, pl.ds(0, LANES)] = part[:FB]
                lead[b, at, pl.ds(LANES, LANES)] = part[FB:]
    spot = (iota((LANES, LANES), 0) + HALF) % LANES
    band = spot - lane % 64
    mask = (band >= 1) & (band <= 64)
    first = iota((1, LANES), 1) < 64
    for b in range(8):
        taps = taps_ref[0, b : b + 1, :]
        swapped = pltpu.roll(taps, 64, 1)
        swapped = jnp.where(first, -swapped, swapped)
        for j, line in enumerate((taps, swapped)):
            spread = jnp.broadcast_to(line, (LANES, LANES))
            spread = pltpu.roll(spread, 96, 1, stride=1, stride_axis=0)
            for k, part in enumerate(split(jnp.where(mask, spread, 0.0))):
                weights[b, pl.ds(j * LANES, LANES), pl.ds(k * LANES, LANES)] = part
    half = iota((FB, LANES), 1) < 64
    for b in range(8):
        rows = pl.ds(b * FB, FB)
        made = mm(lead[b], weights[b])
        made = (made[:LANES, :LANES] + made[LANES:, :LANES]) + (
            made[:LANES, LANES:] + made[LANES:, LANES:]
        )
        made0, made1 = made[:FB], made[FB:]
        real = jnp.where(half, made0, pltpu.roll(made1, 64, 1))
        imag = jnp.where(half, pltpu.roll(made0, 64, 1), made1)
        out_ref[0, 0, rows, :] = r_ref[0, 0, rows, :] - real
        out_ref[0, 1, rows, :] = r_ref[0, 1, rows, :] - imag
    taps_out_ref[0, 0] = taps_ref[0, :, :TAPS]
    taps_out_ref[0, 1] = taps_ref[0, :, TAPS:]


def subtract(multiples, recorded, left, right, taps):
    shots = multiples.shape[0]
    return pl.pallas_call(
        subtract_kernel,
        grid=(shots,),
        in_specs=[
            field_spec(),
            field_spec(),
            edge_spec(),
            edge_spec(),
            pl.BlockSpec((1, 8, LANES), lambda s: (s, 0, 0)),
        ],
        out_specs=[field_spec(), pl.BlockSpec((1, 2, 8, TAPS), lambda s: (s, 0, 0, 0))],
        out_shape=[
            jax.ShapeDtypeStruct(recorded.shape, f32),
            jax.ShapeDtypeStruct((shots, 2, 8, TAPS), f32),
        ],
        scratch_shapes=[
            pltpu.VMEM((8, 256, 256), bf16),
            pltpu.VMEM((8, 256, 256), bf16),
        ],
        name="subtract",
    )(multiples, recorded, left, right, taps)


def number(y, x, c):
    return (y * 4 + x) * 2 + c


def spread(value, axis, step, only=None):
    pairs = []
    for y in range(4):
        for x in range(4):
            for c in range(2):
                at = {"y": y, "x": x}
                to = dict(at)
                to[axis] = (at[axis] + step) % 4
                if only is None or only(y, x):
                    pairs.append((number(y, x, c), number(to["y"], to["x"], c)))
    return lax.ppermute(value, TRACE, pairs)


def across(value, moves):
    pairs = [
        (number(y, a, c), number(y, b, c)) for y in range(4) for a, b in moves for c in range(2)
    ]
    return lax.ppermute(value, TRACE, pairs)


def body(recorded, multiples):
    shots = multiples.shape[0]
    half = shots // 2
    y, x, c = (lax.axis_index(name) for name in TRACE)
    z = lax.axis_index("z")
    place = number(y, x, c)
    on = jnp.where(place == 0, 1, jnp.where(place == 31, 2, 0)).astype(jnp.int32)[None]
    up = [(i, i + 1) for i in range(31)]
    down = [(i + 1, i) for i in range(31)]
    first, last = pack(0, shots, multiples)
    left = lax.ppermute(last, TRACE, up)
    right = lax.ppermute(first, TRACE, down)
    ends = edges(on, first, last)

    ends = ends.reshape(2, half, 8, HALF, LANES)
    other = jnp.where(c == 0, ends[1], ends[0])
    mine = jnp.where(c == 0, ends[0], ends[1])
    mine = mine + lax.ppermute(other, TRACE, [(0, 1), (31, 30)])
    edge = lax.dynamic_index_in_dim(mine, y, 0, keepdims=False)
    for step in range(1, 4):
        sent = lax.dynamic_index_in_dim(mine, (y + step) % 4, 0, keepdims=False)
        edge = edge + spread(sent, "y", step, lambda y, x: (y, x) in ((0, 0), (3, 3)))
    edge = edge + across(edge, ((0, 2), (3, 1)))
    edge = edge + across(edge, ((0, 1), (2, 3), (3, 2), (1, 0)))
    edge = edge.transpose(1, 0, 2).reshape(8 * HALF, LANES)
    along = [[(i, (i - step) % 4) for i in range(4)] for step in range(1, 4)]

    sums = corr(0, shots, multiples, recorded, left, right)
    sums = sums.reshape(2, half, 16, LANES).swapaxes(0, 1)[:, None]
    sums = jnp.broadcast_to(sums, (4, 4, 2, 16, LANES)).reshape(32, 16, LANES)
    sums = lax.all_to_all(sums, TRACE, 0, 0, tiled=True).sum(axis=0)
    own = jnp.concatenate([sums, edge], axis=0)
    parts = [own] + [lax.ppermute(own, "z", pairs) for pairs in along]
    weight = 0.5 * FB * 4096
    taps = solve(weight, z[None], parts)
    taps = lax.all_to_all(
        jnp.broadcast_to(taps[None], (8, 8, LANES)), ("c", "y"), 0, 0, tiled=True
    )
    return tuple(subtract(multiples, recorded, left, right, taps))


def solution(mesh):
    finer = Mesh(mesh.devices.reshape(4, 4, 4, 2), AXES)
    placed = P(None, None, "z", TRACE)
    return jax.shard_map(
        body,
        mesh=finer,
        in_specs=(placed, placed),
        out_specs=(placed, P(None, None, "z", None)),
        check_vma=False,
    )
```

time: 153 us -> 117 us (0.76)
  Pallas kernels: 74.8 us -> 37.5 us
  starting transfers between devices: 12.1 us -> 34.9 us
  blocking collectives: 31.2 us -> 8.94 us
    pallas_call x4 -> x5, Pallas kernels: 74.8 us -> 37.5 us  [the longest x1 13.2 us: subtract(): pl.pallas_call(subtract_kernel, grid=(shots,), in_specs=[field_spec(), fi...]
    all_to_all x1 -> x0, blocking collectives: 20.7 us -> none  [body(): owned = lax.all_to_all(mine, ('y', 'x'), 0, 0, tiled=True).sum(axis=0)]
    ppermute x2 -> x10, starting transfers between devices: 2.01 us -> 17.4 us  [the longest x3 5.72 us: body(): parts = [own] + [lax.ppermute(own, 'z', pairs) for pairs in along]]
    ppermute x2 -> x10, waiting for transfers between devices: 6.37 us -> 17.6 us  [the longest x3 9.12 us: spread(): return lax.ppermute(value, TRACE, pairs)]
    ppermute x1, waiting for transfers between devices: 10.1 us -> 0.01 us  [body(): left = lax.ppermute(last, TRACE, up)]
    all_to_all x1, starting transfers between devices: 5.66 us -> 13.5 us  [body(): sums = lax.all_to_all(sums, TRACE, 0, 0, tiled=True).sum(axis=0)]
    all_to_all x1, waiting for transfers between devices: 11.4 us -> 8.75 us  [body(): sums = lax.all_to_all(sums, TRACE, 0, 0, tiled=True).sum(axis=0)]
    unnamed x6 -> x12, local copies, waits for them, and re-layouts: 1.04 us -> 2.66 us
  transfers between devices with their start and end apart: 4 -> 12, of which waited for: 4 -> 6; matrix products, arithmetic and copies ran while one was open for 0% -> 3% of each run, Pallas kernels for 0% -> 11%
where the time goes in v2:
time: 117 us; the launch traced here: 116 us
  Pallas kernels  37.5 us (32%)
  starting transfers between devices  34.9 us (30%)
  waiting for transfers between devices  26.4 us (23%)
  blocking collectives  8.94 us (8%)
  local copies, waits for them, and re-layouts  5.04 us (4%)
  other arithmetic  2.75 us (2%)
    all_to_all x1, starting transfers between devices, body(): sums = lax.all_to_all(sums, TRACE, 0, 0, tiled=True).sum(axis=0)  13.5 us
    pallas_call x1, Pallas kernels, subtract(): pl.pallas_call(subtract_kernel, grid=(shots,), in_specs=[field_spec(), fi...  13.2 us
    pallas_call x1, Pallas kernels, corr(): pl.pallas_call(lambda *refs: corr_kernel(shots, *refs), grid=(shots,), in...  12.5 us
    ppermute x3, waiting for transfers between devices, spread(): return lax.ppermute(value, TRACE, pairs)  9.12 us
    all_to_all x1, blocking collectives, body(): lax.all_to_all(jnp.broadcast_to(taps[None], (8, 8, LANES)), ('c', 'y'), 0...  8.94 us
    all_to_all x1, waiting for transfers between devices, body(): sums = lax.all_to_all(sums, TRACE, 0, 0, tiled=True).sum(axis=0)  8.75 us
    ppermute x3, waiting for transfers between devices, body(): parts = [own] + [lax.ppermute(own, 'z', pairs) for pairs in along]  5.88 us
    ppermute x3, starting transfers between devices, body(): parts = [own] + [lax.ppermute(own, 'z', pairs) for pairs in along]  5.72 us
  transfers between devices with their start and end apart: 12, of which 6 were waited for; matrix products, arithmetic and copies ran while one was open for 3% of the time, Pallas kernels for 11%

profile of v2, /device:TPU:1, one launch (start us, length us, event | category | flops | bytes accessed | tf_op | source)
XLA Modules:
  0.0 116.4 jit_solution(5550539656435576846)
XLA Ops:
  0.6 4.7 %pack.1 = (f32[8,8,32,128]{3,2,1,0:T(8,128)}, f32[8,8,32,128]{3,2,1,0:T(8,128)}) custom-call(f32[8,2,512,128]{3,2,1,0:T(8,128)} %m_ref.3), custom_call_target="tpu_custom_call" | custom-call | tf_op jit(solution)/shard_map/pack/pallas_call | solution.py:68
  5.4 2.6 %edges.1 = f32[8,8,32,128]{3,2,1,0:T(8,128)} custom-call(s32[1]{0:T(128)} %bitcast.4.refs_0_, f32[8,8,32,128]{3,2,1,0:T(8,128)} %get-tuple-element.5.refs_1_, f32[8,8,32,128]{3,2,1,0:T(8,128)} %get-tuple-element.4.refs_2_), custom_call_target="tpu_custom_call" | custom-call | tf_op jit(solution)/shard_map/edges/pallas_call | solution.py:144
  8.0 1.3 %slice_select_fusion = f32[4,8,32,128]{3,2,1,0:T(8,128)S(1)} fusion(f32[8,8,32,128]{3,2,1,0:T(8,128)} %edges.1, pred[]{:T(512)S(6)} %eq.14), kind=kLoop, calls=%fused_computation.1 | loop fusion | flops 131072 | bytes 1572865 | tf_op jit(solution)/shard_map/jit(_where)/select_n | solution.py:439
  9.3 1.3 %collective-permute-start.2 = (f32[4,8,32,128]{3,2,1,0:T(8,128)S(1)}, f32[4,8,32,128]{3,2,1,0:T(8,128)S(1)}, u32[]{:S(2)}, u32[]{:S(2)}) collective-permute-start(f32[4,8,32,128]{3,2,1,0:T(8,128)S(1)} %slice_select_fusion), channel_id=1, source_target_pairs={{0,1},{31,30},{32,33},{63,62},{64,65},{95,94},{96,97},{127,126}} | collective-permute-start | bytes 1572872 | tf_op jit(solution)/shard_map/ppermute | solution.py:441
  10.6 3.9 %collective-permute-start = (f32[8,8,32,128]{3,2,1,0:T(8,128)}, f32[8,8,32,128]{3,2,1,0:T(8,128)S(1)}, u32[]{:S(2)}, u32[]{:S(2)}) collective-permute-start(f32[8,8,32,128]{3,2,1,0:T(8,128)} %get-tuple-element.4.refs_2_), channel_id=1, source_target_pairs={{0,1},{1,2},{2,3},{3,4},{4,5},{5,6},{6,7},{7,8},{8,9},{9,10},{10,1... | collective-permute-start | bytes 3145736 | tf_op jit(solution)/shard_map/ppermute | solution.py:434
  14.5 5.1 %collective-permute-start.1 = (f32[8,8,32,128]{3,2,1,0:T(8,128)}, f32[8,8,32,128]{3,2,1,0:T(8,128)S(1)}, u32[]{:S(2)}, u32[]{:S(2)}) collective-permute-start(f32[8,8,32,128]{3,2,1,0:T(8,128)} %get-tuple-element.5.refs_1_), channel_id=1, source_target_pairs={{1,0},{2,1},{3,2},{4,3},{5,4},{6,5},{7,6},{8,7},{9,8},{10,9},{11,1... | collective-permute-start | bytes 3145736 | tf_op jit(solution)/shard_map/ppermute | solution.py:435
  19.7 0.0 collective-permute-done.2
  19.7 1.3 %select_add_fusion = f32[4,8,32,128]{3,2,1,0:T(8,128)S(1)} fusion(f32[4,8,32,128]{3,2,1,0:T(8,128)S(1)} %collective-permute-done.2, f32[8,8,32,128]{3,2,1,0:T(8,128)} %edges.1, pred[]{:T(512)S(6)} %eq.14), kind=kLoop, calls=%fused_computation | loop fusion | flops 262144 | bytes 2097153 | tf_op jit(solution)/shard_map/add | solution.py:441
  21.1 1.3 %collective-permute-start.3 = (f32[8,32,128]{2,1,0:T(8,128)S(1)}, f32[8,32,128]{2,1,0:T(8,128)S(1)}, u32[]{:S(2)}, u32[]{:S(2)}) collective-permute-start(f32[8,32,128]{2,1,0:T(8,128)S(1)} %get-tuple-element.6), channel_id=1, source_target_pairs={{0,8},{1,9},{30,6},{31,7},{32,40},{33,41},{62,38},{63,39},{64,72},... | collective-permute-start | bytes 393224 | tf_op jit(solution)/shard_map/ppermute | solution.py:414
  22.4 1.3 %collective-permute-start.5 = (f32[8,32,128]{2,1,0:T(8,128)S(1)}, f32[8,32,128]{2,1,0:T(8,128)S(1)}, u32[]{:S(2)}, u32[]{:S(2)}) collective-permute-start(f32[8,32,128]{2,1,0:T(8,128)S(1)} %get-tuple-element.7), channel_id=1, source_target_pairs={{0,24},{1,25},{30,22},{31,23},{32,56},{33,57},{62,54},{63,55},{64,... | collective-permute-start | bytes 393224 | tf_op jit(solution)/shard_map/ppermute | solution.py:414
  23.7 1.3 %collective-permute-start.4 = (f32[8,32,128]{2,1,0:T(8,128)S(1)}, f32[8,32,128]{2,1,0:T(8,128)S(1)}, u32[]{:S(2)}, u32[]{:S(2)}) collective-permute-start(f32[8,32,128]{2,1,0:T(8,128)S(1)} %get-tuple-element.8), channel_id=1, source_target_pairs={{0,16},{1,17},{30,14},{31,15},{32,48},{33,49},{62,46},{63,47},{64,... | collective-permute-start | bytes 393224 | tf_op jit(solution)/shard_map/ppermute | solution.py:414
  25.0 6.3 %collective-permute-done.3 = f32[8,32,128]{2,1,0:T(8,128)S(1)} collective-permute-done((f32[8,32,128]{2,1,0:T(8,128)S(1)}, f32[8,32,128]{2,1,0:T(8,128)S(1)}, u32[]{:S(2)}, u32[]{:S(2)}) %collective-permute-start.3) | collective-permute-done | bytes 131104 | tf_op jit(solution)/shard_map/ppermute | solution.py:414
  31.3 0.0 collective-permute-done.5
  31.3 2.8 %collective-permute-done.4 = f32[8,32,128]{2,1,0:T(8,128)S(1)} collective-permute-done((f32[8,32,128]{2,1,0:T(8,128)S(1)}, f32[8,32,128]{2,1,0:T(8,128)S(1)}, u32[]{:S(2)}, u32[]{:S(2)}) %collective-permute-start.4) | collective-permute-done | bytes 131104 | tf_op jit(solution)/shard_map/ppermute | solution.py:414
  34.2 1.3 %collective-permute-start.6 = (f32[8,32,128]{2,1,0:T(8,128)S(1)}, f32[8,32,128]{2,1,0:T(8,128)S(1)}, u32[]{:S(2)}, u32[]{:S(2)}) collective-permute-start(f32[8,32,128]{2,1,0:T(8,128)S(1)} %fusion.1), channel_id=1, source_target_pairs={{0,4},{1,5},{6,2},{7,3},{8,12},{9,13},{14,10},{15,11},{16,20},{17,... | collective-permute-start | bytes 393224 | tf_op jit(solution)/shard_map/ppermute | solution.py:421
  35.5 2.6 %collective-permute-done.6 = f32[8,32,128]{2,1,0:T(8,128)S(1)} collective-permute-done((f32[8,32,128]{2,1,0:T(8,128)S(1)}, f32[8,32,128]{2,1,0:T(8,128)S(1)}, u32[]{:S(2)}, u32[]{:S(2)}) %collective-permute-start.6) | collective-permute-done | bytes 131104 | tf_op jit(solution)/shard_map/ppermute | solution.py:421
  38.1 0.1 collective-permute-start.7
  38.2 0.0 collective-permute-done.refs_2_.left_ref
  38.2 0.0 copy-start
  38.2 0.0 collective-permute-done.1.refs_3_.right_ref
  38.3 1.0 copy-done
  39.2 0.0 copy-start.1
  39.2 1.0 copy-done.1
  40.2 12.5 %corr.1 = f32[8,16,128]{2,1,0:T(8,128)} custom-call(f32[8,2,512,128]{3,2,1,0:T(8,128)} %m_ref.3, f32[8,2,512,128]{3,2,1,0:T(8,128)} %r_ref.1, f32[8,8,32,128]{3,2,1,0:T(8,128)} %copy-done, f32[8,8,32,128]{3,2,1,0:T(8,128)} %copy-done.1), custom_call_target="tpu_custom_call" | custom-call | tf_op jit(solution)/shard_map/corr/pallas_call | solution.py:220
  52.7 0.8 copy.7
  53.5 0.7 broadcast_in_dim.9
  54.3 13.5 %all-to-all-start = ((f32[32,16,128]{2,1,0:T(8,128)}), f32[32,16,128]{2,1,0:T(8,128)S(1)}, u32[]{:S(2)}, u32[]{:S(2)}) async-start(f32[32,16,128]{2,1,0:T(8,128)} %bitcast.3), calls=%async_computation | async-start | bytes 524288 | tf_op jit(solution)/shard_map/all_to_all | solution.py:454
  67.8 0.0 collective-permute-done.7
  67.8 0.1 copy.10
  67.9 8.7 %all-to-all-done = f32[32,16,128]{2,1,0:T(8,128)S(1)} async-done(((f32[32,16,128]{2,1,0:T(8,128)}), f32[32,16,128]{2,1,0:T(8,128)S(1)}, u32[]{:S(2)}, u32[]{:S(2)}) %all-to-all-start) | async-done | bytes 262176 | tf_op jit(solution)/shard_map/all_to_all | solution.py:454
  76.7 0.0 copy-start.2
  76.8 1.7 %collective-permute-start.10 = (f32[272,128]{1,0:T(8,128)S(1)}, f32[272,128]{1,0:T(8,128)S(1)}, u32[]{:S(2)}, u32[]{:S(2)}) collective-permute-start(f32[272,128]{1,0:T(8,128)S(1)} %pad_maximum_fusion.refs_1_), channel_id=1, source_target_pairs={{0,32},{32,64},{64,96},{96,0},{1,33},{33,65},{65,97},{97,1},{2,34}... | collective-permute-start | bytes 417800 | tf_op jit(solution)/shard_map/ppermute | solution.py:456
  78.5 3.3 %collective-permute-start.9 = (f32[272,128]{1,0:T(8,128)S(1)}, f32[272,128]{1,0:T(8,128)S(1)}, u32[]{:S(2)}, u32[]{:S(2)}) collective-permute-start(f32[272,128]{1,0:T(8,128)S(1)} %pad_maximum_fusion.refs_1_), channel_id=1, source_target_pairs={{0,64},{32,96},{64,0},{96,32},{1,65},{33,97},{65,1},{97,33},{2,66}... | collective-permute-start | bytes 417800 | tf_op jit(solution)/shard_map/ppermute | solution.py:456
  81.8 0.7 collective-permute-start.8
  82.5 2.0 %collective-permute-done.10.refs_4_ = f32[272,128]{1,0:T(8,128)S(1)} collective-permute-done((f32[272,128]{1,0:T(8,128)S(1)}, f32[272,128]{1,0:T(8,128)S(1)}, u32[]{:S(2)}, u32[]{:S(2)}) %collective-permute-start.10) | collective-permute-done | bytes 139296 | tf_op jit(solution)/shard_map/ppermute | solution.py:456
  84.5 0.0 copy-start.3
  84.5 3.9 %collective-permute-done.9.refs_3_ = f32[272,128]{1,0:T(8,128)S(1)} collective-permute-done((f32[272,128]{1,0:T(8,128)S(1)}, f32[272,128]{1,0:T(8,128)S(1)}, u32[]{:S(2)}, u32[]{:S(2)}) %collective-permute-start.9) | collective-permute-done | bytes 139296 | tf_op jit(solution)/shard_map/ppermute | solution.py:456
  88.4 0.0 copy-start.4
  88.4 0.0 collective-permute-done.8.refs_2_
  88.4 0.0 copy-start.5
  88.4 0.0 copy-done.2
  88.4 0.0 copy-done.3
  88.4 0.6 copy-done.4
  89.0 0.1 copy-done.5
  89.1 4.5 %solve.1 = f32[8,128]{1,0:T(8,128)} custom-call(s32[1]{0:T(128)} %bitcast.refs_0_, f32[272,128]{1,0:T(8,128)} %copy-done.2, f32[272,128]{1,0:T(8,128)} %copy-done.5, f32[272,128]{1,0:T(8,128)} %copy-done.4, f32[272,128]{1,0:T(8,128)} %copy-done.3), custom_call_target="tpu_custom_call" | custom-call | tf_op jit(solution)/shard_map/solve/pallas_call | solution.py:315
  93.6 0.7 broadcast_in_dim.21
  94.3 8.9 %all_to_all.10.taps_ref = f32[8,8,128]{2,1,0:T(8,128)} all-to-all(f32[8,8,128]{2,1,0:T(8,128)S(1)} %broadcast_in_dim.21), channel_id=1, replica_groups=mesh['z'=4,'y'=4,'x'=4,'c'=2] {'c','y'}, dimensions={0} | all-to-all | bytes 65536 | tf_op jit(solution)/shard_map/all_to_all | solution.py:459
  103.2 13.2 %subtract.1 = (f32[8,2,512,128]{3,2,1,0:T(8,128)}, f32[8,2,8,64]{3,2,1,0:T(8,128)}) custom-call(f32[8,2,512,128]{3,2,1,0:T(8,128)} %m_ref.3, f32[8,2,512,128]{3,2,1,0:T(8,128)} %r_ref.1, f32[8,8,32,128]{3,2,1,0:T(8,128)} %copy-done, f32[8,8,32,128]{3,2,1,0:T(8,128)} %copy-done.1, f32[8,8,128]{2,1,0:T(8,128)} %all_to_all.10.taps_ref), custom_call_target="tpu_custom_call" | custom-call | tf_op jit(solution)/shard_map/subtract/pallas_call | solution.py:377
  (6 shorter events, 0.2 us)
Async XLA Ops:
  9.3 10.4 %collective-permute-start.2 = (f32[4,8,32,128]{3,2,1,0:T(8,128)S(1)}, f32[4,8,32,128]{3,2,1,0:T(8,128)S(1)}, u32[]{:S(2)}, u32[]{:S(2)}) collective-permute-start(f32[4,8,32,128]{3,2,1,0:T(8,128)S(1)} %slice_select_fusion), channel_id=1, source_target_pairs={{0,1},{31,30},{32,33},{63,62},{64,65},{95,94},{96,97},{127,126}} | collective-permute-start | bytes 1572872 | tf_op jit(solution)/shard_map/ppermute | solution.py:441
  10.6 27.6 %collective-permute-start = (f32[8,8,32,128]{3,2,1,0:T(8,128)}, f32[8,8,32,128]{3,2,1,0:T(8,128)S(1)}, u32[]{:S(2)}, u32[]{:S(2)}) collective-permute-start(f32[8,8,32,128]{3,2,1,0:T(8,128)} %get-tuple-element.4.refs_2_), channel_id=1, source_target_pairs={{0,1},{1,2},{2,3},{3,4},{4,5},{5,6},{6,7},{7,8},{8,9},{9,10},{10,1... | collective-permute-start | bytes 3145736 | tf_op jit(solution)/shard_map/ppermute | solution.py:434
  14.5 23.7 %collective-permute-start.1 = (f32[8,8,32,128]{3,2,1,0:T(8,128)}, f32[8,8,32,128]{3,2,1,0:T(8,128)S(1)}, u32[]{:S(2)}, u32[]{:S(2)}) collective-permute-start(f32[8,8,32,128]{3,2,1,0:T(8,128)} %get-tuple-element.5.refs_1_), channel_id=1, source_target_pairs={{1,0},{2,1},{3,2},{4,3},{5,4},{6,5},{7,6},{8,7},{9,8},{10,9},{11,1... | collective-permute-start | bytes 3145736 | tf_op jit(solution)/shard_map/ppermute | solution.py:435
  21.1 10.2 %collective-permute-start.3 = (f32[8,32,128]{2,1,0:T(8,128)S(1)}, f32[8,32,128]{2,1,0:T(8,128)S(1)}, u32[]{:S(2)}, u32[]{:S(2)}) collective-permute-start(f32[8,32,128]{2,1,0:T(8,128)S(1)} %get-tuple-element.6), channel_id=1, source_target_pairs={{0,8},{1,9},{30,6},{31,7},{32,40},{33,41},{62,38},{63,39},{64,72},... | collective-permute-start | bytes 393224 | tf_op jit(solution)/shard_map/ppermute | solution.py:414
  22.4 8.9 %collective-permute-start.5 = (f32[8,32,128]{2,1,0:T(8,128)S(1)}, f32[8,32,128]{2,1,0:T(8,128)S(1)}, u32[]{:S(2)}, u32[]{:S(2)}) collective-permute-start(f32[8,32,128]{2,1,0:T(8,128)S(1)} %get-tuple-element.7), channel_id=1, source_target_pairs={{0,24},{1,25},{30,22},{31,23},{32,56},{33,57},{62,54},{63,55},{64,... | collective-permute-start | bytes 393224 | tf_op jit(solution)/shard_map/ppermute | solution.py:414
  23.7 10.4 %collective-permute-start.4 = (f32[8,32,128]{2,1,0:T(8,128)S(1)}, f32[8,32,128]{2,1,0:T(8,128)S(1)}, u32[]{:S(2)}, u32[]{:S(2)}) collective-permute-start(f32[8,32,128]{2,1,0:T(8,128)S(1)} %get-tuple-element.8), channel_id=1, source_target_pairs={{0,16},{1,17},{30,14},{31,15},{32,48},{33,49},{62,46},{63,47},{64,... | collective-permute-start | bytes 393224 | tf_op jit(solution)/shard_map/ppermute | solution.py:414
  34.2 3.9 %collective-permute-start.6 = (f32[8,32,128]{2,1,0:T(8,128)S(1)}, f32[8,32,128]{2,1,0:T(8,128)S(1)}, u32[]{:S(2)}, u32[]{:S(2)}) collective-permute-start(f32[8,32,128]{2,1,0:T(8,128)S(1)} %fusion.1), channel_id=1, source_target_pairs={{0,4},{1,5},{6,2},{7,3},{8,12},{9,13},{14,10},{15,11},{16,20},{17,... | collective-permute-start | bytes 393224 | tf_op jit(solution)/shard_map/ppermute | solution.py:421
  38.1 29.7 %collective-permute-start.7 = (f32[8,32,128]{2,1,0:T(8,128)S(1)}, f32[8,32,128]{2,1,0:T(8,128)S(1)}, u32[]{:S(2)}, u32[]{:S(2)}) collective-permute-start(f32[8,32,128]{2,1,0:T(8,128)S(1)} %add.72), channel_id=1, source_target_pairs={{0,2},{1,3},{4,6},{5,7},{6,4},{7,5},{2,0},{3,1},{8,10},{9,11},{12,... | collective-permute-start | bytes 393224 | tf_op jit(solution)/shard_map/ppermute | solution.py:421
  38.2 1.0 copy-start
  39.2 1.0 copy-start.1
  54.3 22.4 %all-to-all-start = ((f32[32,16,128]{2,1,0:T(8,128)}), f32[32,16,128]{2,1,0:T(8,128)S(1)}, u32[]{:S(2)}, u32[]{:S(2)}) async-start(f32[32,16,128]{2,1,0:T(8,128)} %bitcast.3), calls=%async_computation | async-start | bytes 524288 | tf_op jit(solution)/shard_map/all_to_all | solution.py:454
  76.7 11.6 %copy-start.2 = (f32[272,128]{1,0:T(8,128)}, f32[272,128]{1,0:T(8,128)S(1)}, u32[]{:S(2)}) copy-start(f32[272,128]{1,0:T(8,128)S(1)} %pad_maximum_fusion.refs_1_) | copy-start | bytes 417796
  76.8 7.7 %collective-permute-start.10 = (f32[272,128]{1,0:T(8,128)S(1)}, f32[272,128]{1,0:T(8,128)S(1)}, u32[]{:S(2)}, u32[]{:S(2)}) collective-permute-start(f32[272,128]{1,0:T(8,128)S(1)} %pad_maximum_fusion.refs_1_), channel_id=1, source_target_pairs={{0,32},{32,64},{64,96},{96,0},{1,33},{33,65},{65,97},{97,1},{2,34}... | collective-permute-start | bytes 417800 | tf_op jit(solution)/shard_map/ppermute | solution.py:456
  78.5 9.9 %collective-permute-start.9 = (f32[272,128]{1,0:T(8,128)S(1)}, f32[272,128]{1,0:T(8,128)S(1)}, u32[]{:S(2)}, u32[]{:S(2)}) collective-permute-start(f32[272,128]{1,0:T(8,128)S(1)} %pad_maximum_fusion.refs_1_), channel_id=1, source_target_pairs={{0,64},{32,96},{64,0},{96,32},{1,65},{33,97},{65,1},{97,33},{2,66}... | collective-permute-start | bytes 417800 | tf_op jit(solution)/shard_map/ppermute | solution.py:456
  81.8 6.6 %collective-permute-start.8 = (f32[272,128]{1,0:T(8,128)S(1)}, f32[272,128]{1,0:T(8,128)S(1)}, u32[]{:S(2)}, u32[]{:S(2)}) collective-permute-start(f32[272,128]{1,0:T(8,128)S(1)} %pad_maximum_fusion.refs_1_), channel_id=1, source_target_pairs={{0,96},{32,0},{64,32},{96,64},{1,97},{33,1},{65,33},{97,65},{2,98}... | collective-permute-start | bytes 417800 | tf_op jit(solution)/shard_map/ppermute | solution.py:456
  84.5 3.9 %copy-start.3 = (f32[272,128]{1,0:T(8,128)}, f32[272,128]{1,0:T(8,128)S(1)}, u32[]{:S(2)}) copy-start(f32[272,128]{1,0:T(8,128)S(1)} %collective-permute-done.10.refs_4_) | copy-start | bytes 417796
  88.4 0.6 copy-start.4
  88.4 0.7 copy-start.5
